TPU v7x, 32 devices: a whole 2x2x4 slice. The times are simulated.
32 devices in a mesh: sweep: 1, dp: 8 (over z, y), tensor: 4 (over x, core).
Axes of the slice: x: 2, y: 2, z: 4, core: 2. Of those that a mesh axis runs over, the one named last changes fastest.
Arguments:
- checkpoint: bfloat16 [1024, 8192], P(('sweep', 'dp'), 'tensor'), may hold values from -6 to 6
- norm_gain: bfloat16 [8192], P(('sweep', 'tensor')), may hold values from 0.5 to 1.5
- w_query: bfloat16 [8192, 4096], P(('sweep', 'dp'), 'tensor'), may hold values from -1 to 1
- w_key: bfloat16 [8192, 512], P(('sweep', 'dp'), 'tensor'), may hold values from -8 to 8
- w_value: bfloat16 [8192, 512], P(('sweep', 'dp'), 'tensor'), may hold values from -0.0625 to 0.0625
- grad_attn: bfloat16 [1024, 4096], P(('sweep', 'dp'), 'tensor'), may hold values from -6 to 6
Outputs:
- d_checkpoint: bfloat16 [1024, 8192], P(('sweep', 'dp'), 'tensor')
- grad_gain: float32 [8192], P(('sweep', 'tensor'))
- grad_query: float32 [8192, 4096], P(('sweep', 'dp'), 'tensor')
- grad_key: float32 [8192, 512], P(('sweep', 'dp'), 'tensor')
- grad_value: float32 [8192, 512], P(('sweep', 'dp'), 'tensor')
All inputs are finite; a program needn't handle non-finite values.
Results may differ from a plain program's by a relative error of at most 0.025.
The roundings to bfloat16 on the way count: a program that leaves them out, or rounds other values in their place, can miss the bound.
Values may be sent and summed in bfloat16 or wider, within the bound.
No kernel may reach another device: no remote copies, remote signals or barrier semaphores. Data moves between devices by JAX's collectives and lax.ppermute only.
A program may use at most 128 MiB of HBM per device.

v0:
```python
import jax
import jax.numpy as jnp
from jax import lax
from jax.sharding import PartitionSpec as P

QHEADS = 32
KVHEADS = 4
HD = 128
EPS = 1e-05
THETA = 500000.0


def round_half(field):
    return lax.optimization_barrier(field.astype(jnp.bfloat16))


def angles(positions, head_width):
    frequency = THETA ** (-(jnp.arange(head_width // 2, dtype=jnp.float32) * 2.0) / head_width)
    turned = positions.astype(jnp.float32)[:, None] * frequency[None, :]
    return (jnp.cos(turned)[:, None, :], jnp.sin(turned)[:, None, :])


def rotate(field, cosine_table, sine_table):
    half_width = field.shape[-1] // 2
    front_half = field[..., :half_width]
    back_half = field[..., half_width:]
    return jnp.concatenate(
        [
            front_half * cosine_table - back_half * sine_table,
            back_half * cosine_table + front_half * sine_table,
        ],
        -1,
    )


def rotate_back(field, cosine_table, sine_table):
    half_width = field.shape[-1] // 2
    front_half = field[..., :half_width]
    back_half = field[..., half_width:]
    return jnp.concatenate(
        [
            front_half * cosine_table + back_half * sine_table,
            back_half * cosine_table - front_half * sine_table,
        ],
        -1,
    )


def project_back(grads, matrix):
    return jnp.einsum("tc,dc->td", grads, matrix, preferred_element_type=jnp.float32)


def on_device(checkpoint, norm_gain, w_query, w_key, w_value, grad_attn):
    row_count = checkpoint.shape[0]
    head_width = HD
    group_size = QHEADS // KVHEADS
    full_x, full_gain = (
        lax.all_gather(checkpoint, "tensor", axis=1, tiled=True),
        lax.all_gather(norm_gain, "tensor", axis=0, tiled=True),
    )
    x_wide = full_x.astype(jnp.float32)
    gain_wide = full_gain.astype(jnp.float32)
    model_width = full_x.shape[1]
    inverse = lax.rsqrt(jnp.mean(x_wide * x_wide, -1, keepdims=True) + EPS)
    normed = (x_wide * inverse * gain_wide).astype(jnp.bfloat16)
    query_all, key_all, value_all = (
        lax.all_gather(w_query, "dp", axis=0, tiled=True),
        lax.all_gather(w_key, "dp", axis=0, tiled=True),
        lax.all_gather(w_value, "dp", axis=0, tiled=True),
    )
    q_heads = query_all.shape[1] // head_width
    own_kv = max(1, q_heads // group_size)
    run_heads = q_heads // own_kv
    first_kv = lax.axis_index("tensor") * q_heads // group_size
    queries = jnp.dot(normed, query_all, preferred_element_type=jnp.float32).reshape(
        row_count, q_heads, head_width
    )
    key_local = jnp.dot(normed, key_all, preferred_element_type=jnp.float32)
    value_local = jnp.dot(normed, value_all, preferred_element_type=jnp.float32)
    key_cols_all, value_cols_all = (
        lax.all_gather(key_local, "tensor", axis=1, tiled=True),
        lax.all_gather(value_local, "tensor", axis=1, tiled=True),
    )
    kv_total = key_cols_all.shape[1] // head_width
    first_row = lax.axis_index("dp") * row_count
    own_positions = first_row + jnp.arange(row_count, dtype=jnp.int32)
    cosine_table, sine_table = angles(own_positions, head_width)
    query_rot = rotate(queries, cosine_table, sine_table).astype(jnp.bfloat16)
    key_heads = lax.dynamic_slice_in_dim(
        key_cols_all.reshape(row_count, head_width, kv_total), first_kv, own_kv, 2
    )
    value_heads = lax.dynamic_slice_in_dim(
        value_cols_all.reshape(row_count, head_width, kv_total), first_kv, own_kv, 2
    )
    key_turned = rotate(jnp.transpose(key_heads, (0, 2, 1)), cosine_table, sine_table)
    key_rot = key_turned.astype(jnp.bfloat16).reshape(row_count, own_kv * head_width)
    value_half = (
        jnp.transpose(value_heads, (0, 2, 1))
        .astype(jnp.bfloat16)
        .reshape(row_count, own_kv * head_width)
    )
    gathered_keys, gathered_values = (
        lax.all_gather(key_rot, "dp", axis=0, tiled=True),
        lax.all_gather(value_half, "dp", axis=0, tiled=True),
    )
    seq_length = gathered_keys.shape[0]
    keys_three = gathered_keys.reshape(seq_length, own_kv, head_width)
    values_three = gathered_values.reshape(seq_length, own_kv, head_width)
    score_scale = head_width ** (-0.5)
    query_grp = query_rot.reshape(row_count, own_kv, run_heads, head_width)
    upstream = grad_attn.reshape(row_count, own_kv, run_heads, head_width)
    scores = (
        jnp.einsum("tkgd,skd->kgts", query_grp, keys_three, preferred_element_type=jnp.float32)
        * score_scale
    )
    allowed = own_positions[:, None] >= jnp.arange(seq_length, dtype=jnp.int32)[None, :]
    scores = jnp.where(allowed, scores, -jnp.inf)
    row_top = jnp.max(scores, -1, keepdims=True)
    raw_weights = jnp.exp(scores - row_top)
    chances = raw_weights / jnp.sum(raw_weights, -1, keepdims=True)
    chances_half = chances.astype(jnp.bfloat16)
    attended = jnp.einsum(
        "kgts,skd->tkgd", chances_half, values_three, preferred_element_type=jnp.float32
    )
    row_delta = jnp.sum(upstream.astype(jnp.float32) * attended, -1)
    prob_grads = jnp.einsum(
        "tkgd,skd->kgts", upstream, values_three, preferred_element_type=jnp.float32
    )
    dscore = chances * (prob_grads - jnp.transpose(row_delta, (1, 2, 0))[..., None])
    dscore_half = dscore.astype(jnp.bfloat16)
    dquery = (
        jnp.einsum("kgts,skd->tkgd", dscore_half, keys_three, preferred_element_type=jnp.float32)
        * score_scale
    )
    dkey_part = (
        jnp.einsum("kgts,tkgd->skd", dscore_half, query_grp, preferred_element_type=jnp.float32)
        * score_scale
    )
    dvalue_part = jnp.einsum(
        "kgts,tkgd->skd", chances_half, upstream, preferred_element_type=jnp.float32
    )
    dkey_sum, dvalue_sum = (
        lax.psum_scatter(
            dkey_part.reshape(seq_length, own_kv * head_width).astype(jnp.bfloat16),
            "dp",
            scatter_dimension=0,
            tiled=True,
        ).astype(jnp.float32),
        lax.psum_scatter(
            dvalue_part.reshape(seq_length, own_kv * head_width).astype(jnp.bfloat16),
            "dp",
            scatter_dimension=0,
            tiled=True,
        ).astype(jnp.float32),
    )
    dkey_back = rotate_back(
        dkey_sum.reshape(row_count, own_kv, head_width), cosine_table, sine_table
    )
    dvalue_back = dvalue_sum.reshape(row_count, own_kv, head_width)
    empty_heads = jnp.zeros((row_count, kv_total, head_width), jnp.float32)
    zero_start = jnp.zeros((), jnp.int32)
    dkey_embed = lax.dynamic_update_slice(
        empty_heads, dkey_back, (zero_start, first_kv, zero_start)
    )
    dvalue_embed = lax.dynamic_update_slice(
        empty_heads, dvalue_back, (zero_start, first_kv, zero_start)
    )
    dkey_embed = jnp.transpose(dkey_embed, (0, 2, 1)).reshape(row_count, head_width * kv_total)
    dvalue_embed = jnp.transpose(dvalue_embed, (0, 2, 1)).reshape(row_count, head_width * kv_total)
    dkey_cols, dvalue_cols = (
        lax.psum_scatter(
            dkey_embed.astype(jnp.bfloat16), "tensor", scatter_dimension=1, tiled=True
        ).astype(jnp.float32),
        lax.psum_scatter(
            dvalue_embed.astype(jnp.bfloat16), "tensor", scatter_dimension=1, tiled=True
        ).astype(jnp.float32),
    )
    dquery_pre = (
        rotate_back(dquery.reshape(row_count, q_heads, head_width), cosine_table, sine_table)
        .astype(jnp.bfloat16)
        .reshape(row_count, q_heads * head_width)
    )
    dkey_pre = dkey_cols.astype(jnp.bfloat16)
    dvalue_pre = dvalue_cols.astype(jnp.bfloat16)
    partial_input = (
        project_back(dquery_pre, query_all)
        + project_back(dkey_pre, key_all)
        + project_back(dvalue_pre, value_all)
    )
    slice_width = checkpoint.shape[1]
    x_own = checkpoint.astype(jnp.float32)
    gain_own = norm_gain.astype(jnp.float32)
    input_full = lax.psum(partial_input.astype(jnp.bfloat16), "tensor").astype(jnp.float32)
    row_sum = jnp.sum(gain_wide * input_full * x_wide, -1, keepdims=True)
    input_own = lax.dynamic_slice_in_dim(
        input_full, lax.axis_index("tensor") * slice_width, slice_width, 1
    )
    d_checkpoint = (
        inverse * gain_own * input_own - x_own * inverse**3 * row_sum / model_width
    ).astype(jnp.bfloat16)
    grad_gain = lax.psum(jnp.sum(input_own * x_own * inverse, 0), "dp")
    token_grads = jnp.concatenate([dquery_pre, dkey_pre, dvalue_pre], 1)
    own_rows = w_query.shape[0]
    feature_cols = lax.all_to_all(normed, "dp", split_axis=1, concat_axis=0, tiled=True)
    piece = lax.all_gather(token_grads, "dp", axis=0, tiled=True)
    piece_rows = piece.shape[0]
    blocks = piece_rows // row_count
    block_x = feature_cols.reshape(blocks, row_count, own_rows)
    block_g = piece.reshape(blocks, row_count, piece.shape[1])
    terms = jnp.einsum("btd,btc->bdc", block_x, block_g, preferred_element_type=jnp.float32)
    weight_grads = jnp.sum(round_half(terms).astype(jnp.float32), 0)
    query_cols = w_query.shape[1]
    key_cols = w_key.shape[1]
    grad_query = weight_grads[:, :query_cols]
    grad_key = weight_grads[:, query_cols : query_cols + key_cols]
    grad_value = weight_grads[:, query_cols + key_cols :]
    return (d_checkpoint, grad_gain, grad_query, grad_key, grad_value)


def solution(mesh):
    return jax.shard_map(
        on_device,
        mesh=mesh,
        in_specs=(
            P(("sweep", "dp"), "tensor"),
            P(("sweep", "tensor")),
            P(("sweep", "dp"), "tensor"),
            P(("sweep", "dp"), "tensor"),
            P(("sweep", "dp"), "tensor"),
            P(("sweep", "dp"), "tensor"),
        ),
        out_specs=(
            P(("sweep", "dp"), "tensor"),
            P(("sweep", "tensor")),
            P(("sweep", "dp"), "tensor"),
            P(("sweep", "dp"), "tensor"),
            P(("sweep", "dp"), "tensor"),
        ),
        check_vma=False,
    )
```

profile of v0, /device:TPU:0, one launch (start us, length us, event | category | flops | bytes accessed | tf_op | source)
XLA Modules:
  0.0 710.5 jit_solution(5812037475579603408)
XLA Ops:
  7.2 0.7 all-gather.7.cloned.1.call-update
  7.9 0.7 all-gather.13.cloned.1.call-update
  8.7 0.7 all-gather.9.cloned.1.call-update
  9.4 0.5 all-gather.11.cloned.1.call-update
  10.0 6.4 all_gather.31
  16.4 1.1 copy.55
  17.6 0.3 multiply_cosine_fusion
  18.0 16.9 %all-gather.7.cloned.1.call-done = bf16[128,8192]{1,0:T(8,128)(2,1)} async-done(((bf16[128,2048]{1,0:T(8,128)(2,1)}), bf16[128,8192]{1,0:T(8,128)(2,1)}) %all-gather.7.cloned.1.call-update) | async-done | bytes 2097168 | tf_op jit(solution)/shard_map/all_gather | solution.py:58
  34.9 2.1 fusion.1
  36.9 2.2 fusion.3
  39.1 47.0 %all-gather.13.cloned.1.call-done = bf16[8192,128]{1,0:T(8,128)(2,1)} async-done(((bf16[1024,128]{1,0:T(8,128)(2,1)}), bf16[8192,128]{1,0:T(8,128)(2,1)}) %all-gather.13.cloned.1.call-update) | async-done | bytes 2097168 | tf_op jit(solution)/shard_map/all_gather | solution.py:69
  86.1 2.3 fusion.90
  88.4 5.4 all_gather.37
  94.2 41.7 %all-gather.9.cloned.1.call-done = bf16[8192,128]{1,0:T(8,128)(2,1)} async-done(((bf16[1024,128]{1,0:T(8,128)(2,1)}), bf16[8192,128]{1,0:T(8,128)(2,1)}) %all-gather.9.cloned.1.call-update) | async-done | bytes 2097168 | tf_op jit(solution)/shard_map/all_gather | solution.py:68
  135.9 2.3 fusion.89
  138.2 5.8 all_gather.33
  144.2 0.3 fusion.81
  144.7 32.5 %all_gather.34 = bf16[1024,128]{1,0:T(8,128)(2,1)S(1)} all-gather(bf16[128,128]{1,0:T(8,128)(2,1)S(1)} %pad_maximum_fusion.6), channel_id=1, replica_groups=mesh['sweep'=1,'dp'=8,'tensor'=4] {'dp'}, dimensions={0}, use_global_device_ids=true | all-gather | bytes 294912 | tf_op jit(solution)/shard_map/all_gather | solution.py:103
  177.2 34.9 %all-gather = bf16[1024,128,1]{1,0,2:T(8,128)(2,1)} all-gather(bf16[128,128,1]{1,0,2:T(8,128)(2,1)S(1)} %copy.84), channel_id=2, replica_groups=mesh['sweep'=1,'dp'=8,'tensor'=4] {'dp'}, dimensions={0}, use_global_device_ids=true | all-gather | bytes 294912 | tf_op jit(solution)/shard_map/all_gather | solution.py:104
  212.1 155.9 %all-gather.11.cloned.1.call-done = bf16[8192,1024]{1,0:T(8,128)(2,1)} async-done(((bf16[1024,1024]{1,0:T(8,128)(2,1)}), bf16[8192,1024]{1,0:T(8,128)(2,1)}) %all-gather.11.cloned.1.call-update) | async-done | bytes 16777232 | tf_op jit(solution)/shard_map/all_gather | solution.py:67
  368.0 8.1 %convolution_bitcast_fusion = f32[16,8,8,128]{3,1,2,0:T(8,128)S(1)} fusion(bf16[128,8192]{1,0:T(8,128)(2,1)S(1)} %fusion.3, bf16[8192,1024]{1,0:T(8,128)(2,1)} %all-gather.11.cloned.1.call-done), kind=kOutput, calls=%fused_computation.37 | convolution fusion | flops 2147483648 | bytes 19398656 | tf_op jit(solution)/shard_map/dot_general | solution.py:75
  376.2 0.2 fusion.88
  376.4 0.2 subtract_convert_fusion.1
  376.6 0.8 fusion.9
  377.4 0.9 fusion.8
  378.3 1.3 fusion.47
  379.6 1.5 fusion.6
  381.1 1.3 copy-done.4
  382.4 1.5 fusion.50
  383.9 2.5 fusion.32
  386.5 0.3 add_convert_fusion
  386.7 0.1 pad_maximum_fusion.2
  386.9 0.2 copy.61
  387.1 4.0 fusion.41
  391.2 56.3 %reduce-scatter.5.cloned.1.call-done = bf16[128,128]{1,0:T(8,128)(2,1)} async-done(((bf16[1024,128]{1,0:T(8,128)(2,1)}), bf16[128,128]{1,0:T(8,128)(2,1)}) %reduce-scatter.5.cloned.1.call-update) | async-done | bytes 32784 | tf_op jit(solution)/shard_map/reduce_scatter | solution.py:143
  447.5 0.8 bitcast_convert_fusion.1
  448.3 0.3 fusion.78
  448.7 0.1 copy.65
  448.9 1.4 dynamic_update_slice.6
  450.3 0.6 copy-done.6
  451.0 0.3 reduce-scatter.11.cloned.1.call-start
  451.3 13.5 %fusion.91 = f32[128,8192]{1,0:T(8,128)} fusion(bf16[128,1024]{0,1:T(8,128)(2,1)S(1)} %bitcast.168, bf16[8192,1024]{1,0:T(8,128)(2,1)} %all-gather.11.cloned.1.call-done), kind=kOutput, calls=%fused_computation.102 | convolution fusion | flops 2147483648 | bytes 21233664 | tf_op jit(solution)/shard_map/tc,dc->td/dot_general | solution.py:50
  464.8 47.7 %reduce-scatter.9.cloned.1.call-done = bf16[128,128]{1,0:T(8,128)(2,1)} async-done(((bf16[1024,128]{1,0:T(8,128)(2,1)}), bf16[128,128]{1,0:T(8,128)(2,1)}) %reduce-scatter.9.cloned.1.call-update) | async-done | bytes 32784 | tf_op jit(solution)/shard_map/reduce_scatter | solution.py:149
  512.5 0.9 copy.67
  513.4 1.4 dynamic_update_slice.7
  514.8 0.6 copy-done.5
  515.6 18.7 %reduce-scatter.7.cloned.1.call-done = bf16[128,128]{0,1:T(8,128)(2,1)} async-done(((bf16[128,512]{0,1:T(8,128)(2,1)}), bf16[128,128]{0,1:T(8,128)(2,1)}) %reduce-scatter.7.cloned.1.call-update) | async-done | bytes 32784 | tf_op jit(solution)/shard_map/reduce_scatter | solution.py:171
  534.2 5.6 convolution_add_fusion.1
  539.8 17.1 %reduce-scatter.11.cloned.1.call-done = bf16[128,128]{0,1:T(8,128)(2,1)} async-done(((bf16[128,512]{0,1:T(8,128)(2,1)}), bf16[128,128]{0,1:T(8,128)(2,1)}) %reduce-scatter.11.cloned.1.call-update) | async-done | bytes 32784 | tf_op jit(solution)/shard_map/reduce_scatter | solution.py:174
  556.9 4.9 fusion
  561.9 0.7 pad_maximum_fusion
  562.7 2.4 copy.81
  565.2 5.5 all-to-all-start
  570.7 42.7 %all-reduce.2.cloned.1.call-done = bf16[128,8192]{1,0:T(8,128)(2,1)} async-done(((bf16[128,8192]{1,0:T(8,128)(2,1)}), bf16[128,8192]{1,0:T(8,128)(2,1)}) %all-reduce.2.cloned.1.call-update) | async-done | bytes 2097168 | tf_op jit(solution)/shard_map/psum | solution.py:193
  613.4 2.2 convert_element_type.142
  615.6 0.8 fusion.4
  616.4 1.4 fusion.58
  617.8 23.2 %psum.15 = f32[2048]{0:T(1024)} all-reduce(f32[2048]{0:T(1024)S(1)} %get-tuple-element.7), channel_id=1, replica_groups=mesh['sweep'=1,'dp'=8,'tensor'=4] {'dp'}, use_global_device_ids=true, to_apply=%region_11.12 | all-reduce | flops 2048 | bytes 16384 | tf_op jit(solution)/shard_map/psum | solution.py:201
  641.0 31.3 %all-gather.15.cloned.1.call-done = bf16[1024,1280]{0,1:T(8,128)(2,1)} async-done(((bf16[128,1280]{0,1:T(8,128)(2,1)}), bf16[1024,1280]{0,1:T(8,128)(2,1)}) %all-gather.15.cloned.1.call-update) | async-done | bytes 2621456 | tf_op jit(solution)/shard_map/all_gather | solution.py:205
  672.4 4.4 copy.69
  676.7 11.9 %convolution_convert_fusion = bf16[8,1024,1280]{2,1,0:T(8,128)(2,1)} fusion(bf16[8,128,1280]{2,1,0:T(8,128)(2,1)} %bitcast.165, bf16[128,8,1024]{0,2,1:T(8,128)(2,1)} %all-to-all-done), kind=kOutput, calls=%fused_computation.1 | convolution fusion | flops 2694840320 | bytes 25690112 | tf_op jit(solution)/shard_map/btd,btc->bdc/dot_general | solution.py:210
  688.7 11.3 %convert_reduce_fusion = f32[1024,1280]{1,0:T(8,128)S(1)} fusion(bf16[8,1024,1280]{2,1,0:T(8,128)(2,1)} %convolution_convert_fusion), kind=kLoop, calls=%fused_computation | loop fusion | flops 19660800 | bytes 26214400 | tf_op jit(solution)/shard_map/reduce_sum | solution.py:211
  699.9 1.0 fusion.87
  701.0 2.7 slice.52
  (55 shorter events, 1.6 us)
Async XLA Ops:
  7.2 27.7 %all-gather.7.cloned.1.call-start = ((), (), s32[]{:S(2)}) async-start(), calls=%async_computation.5 | async-start | bytes 2621440 | tf_op jit(solution)/shard_map/all_gather | solution.py:58
  7.9 78.2 %all-gather.13.cloned.1.call-start = ((), (), s32[]{:S(2)}) async-start(), calls=%async_computation.8 | async-start | bytes 2359296 | tf_op jit(solution)/shard_map/all_gather | solution.py:69
  8.6 127.2 %all-gather.9.cloned.1.call-start = ((), (), s32[]{:S(2)}) async-start(), calls=%async_computation.6 | async-start | bytes 2359296 | tf_op jit(solution)/shard_map/all_gather | solution.py:68
  9.4 358.6 %all-gather.11.cloned.1.call-start = ((), (), s32[]{:S(2)}) async-start(), calls=%async_computation.7 | async-start | bytes 18874368 | tf_op jit(solution)/shard_map/all_gather | solution.py:67
  10.0 437.6 %reduce-scatter.5.cloned.1.call-start = ((), (), s32[]{:S(2)}) async-start(), calls=%async_computation.9 | async-start | bytes 294912 | tf_op jit(solution)/shard_map/reduce_scatter | solution.py:143
  376.6 1.7 copy-start.8
  377.4 2.2 copy-start.1
  378.3 1.3 copy-start.7
  381.1 1.3 copy-start.4
  387.1 125.4 %reduce-scatter.9.cloned.1.call-start = ((), (), s32[]{:S(2)}) async-start(), calls=%async_computation.11 | async-start | bytes 294912 | tf_op jit(solution)/shard_map/reduce_scatter | solution.py:149
  391.2 143.0 %reduce-scatter.7.cloned.1.call-start = ((), (), s32[]{:S(2)}) async-start(), calls=%async_computation.10 | async-start | bytes 163840 | tf_op jit(solution)/shard_map/reduce_scatter | solution.py:171
  450.3 0.7 copy-start.6
  451.0 105.9 %reduce-scatter.11.cloned.1.call-start = ((), (), s32[]{:S(2)}) async-start(), calls=%async_computation.12 | async-start | bytes 163840 | tf_op jit(solution)/shard_map/reduce_scatter | solution.py:174
  514.8 0.7 copy-start.5
  515.5 97.9 %all-reduce.2.cloned.1.call-start = ((), (), s32[]{:S(2)}) async-start(), calls=%async_computation.13 | async-start | bytes 4194304 | tf_op jit(solution)/shard_map/psum | solution.py:193
  539.8 22.1 %copy-start.9 = (bf16[128,128]{0,1:T(8,128)(2,1)S(1)}, bf16[128,128]{0,1:T(8,128)(2,1)}, u32[]{:S(2)}) copy-start(bf16[128,128]{0,1:T(8,128)(2,1)} %reduce-scatter.7.cloned.1.call-done) | copy-start | bytes 98308
  556.9 5.0 copy-start.10
  561.9 110.5 %all-gather.15.cloned.1.call-start = ((), (), s32[]{:S(2)}) async-start(), calls=%async_computation.14 | async-start | bytes 2949120 | tf_op jit(solution)/shard_map/all_gather | solution.py:205
  562.7 8.0 %copy-start.11 = (bf16[2048]{0:T(1024)(128)(2,1)S(1)}, bf16[2048]{0:T(1024)(128)(2,1)}, u32[]{:S(2)}) copy-start(bf16[2048]{0:T(1024)(128)(2,1)} %param.7) | copy-start | bytes 12292
  565.2 111.6 %all-to-all-start = ((bf16[128,8,1024]{0,2,1:T(8,128)(2,1)}), bf16[128,8,1024]{0,2,1:T(8,128)(2,1)}, u32[]{:S(2)}, u32[]{:S(2)}) async-start(bf16[128,8,1024]{0,2,1:T(8,128)(2,1)} %bitcast.166), calls=%async_computation.4 | async-start | bytes 4194304 | tf_op jit(solution)/shard_map/all_to_all | solution.py:204
  570.7 44.9 %copy-start = (bf16[128,8192]{1,0:T(8,128)(2,1)S(1)}, bf16[128,8192]{1,0:T(8,128)(2,1)}, u32[]{:S(2)}) copy-start(bf16[128,8192]{1,0:T(8,128)(2,1)} %all-gather.7.cloned.1.call-done) | copy-start | bytes 6291460
  570.7 45.7 %copy-start.3 = (bf16[128,2048]{1,0:T(8,128)(2,1)S(1)}, bf16[128,2048]{1,0:T(8,128)(2,1)}, u32[]{:S(2)}) copy-start(bf16[128,2048]{1,0:T(8,128)(2,1)} %param.6) | copy-start | bytes 1572868
  613.4 2.2 copy-start.2
Sparse Core Ops, SparseCore 0:
  9.5 25.2 all-gather.6
  37.0 49.0 all-gather.12
  88.2 47.6 all-gather.8
  137.9 230.0 all-gather.10
  387.2 60.2 reduce-scatter.4
  451.3 61.1 reduce-scatter.8
  515.5 18.7 reduce-scatter.6
  537.2 19.6 reduce-scatter.10
  562.0 51.3 all-reduce.1
  615.9 56.4 all-gather.14
where the time goes:
time: 711 us; the launch traced here: 710 us
  waiting for transfers between devices  478 us (67%)
  blocking collectives  108 us (15%)
  matrix products  60.2 us (8%)
  other arithmetic  24.1 us (3%)
  local copies, waits for them, and re-layouts  19.3 us (3%)
  between operations  14.6 us (2%)
    all_gather x1, waiting for transfers between devices, on_device(): lax.all_gather(w_query, 'dp', axis=0, tiled=True)  156 us
    reduce_scatter x1, waiting for transfers between devices, on_device(): lax.psum_scatter(dkey_part.reshape(seq_length, own_kv * head_width).astyp...  56.3 us
    reduce_scatter x1, waiting for transfers between devices, on_device(): lax.psum_scatter(dvalue_part.reshape(seq_length, own_kv * head_width).ast...  47.7 us
    all_gather x1, waiting for transfers between devices, on_device(): lax.all_gather(w_value, 'dp', axis=0, tiled=True)  47 us
    psum x1, waiting for transfers between devices, on_device(): lax.psum(partial_input.astype(jnp.bfloat16), 'tensor').astype(jnp.float32)  42.7 us
    all_gather x1, waiting for transfers between devices, on_device(): lax.all_gather(w_key, 'dp', axis=0, tiled=True)  41.7 us
    all_gather x1, blocking collectives, on_device(): lax.all_gather(value_half, 'dp', axis=0, tiled=True)  34.9 us
    all_gather x1, blocking collectives, on_device(): lax.all_gather(key_rot, 'dp', axis=0, tiled=True)  32.5 us
  transfers between devices with their start and end apart: 11, of which 10 were waited for; matrix products, arithmetic and copies ran while one was open for 7% of the time, Pallas kernels for 0%

commit v1 on v0

--- a/solution.py
+++ b/solution.py
@@ -190,7 +190,12 @@
     slice_width = checkpoint.shape[1]
     x_own = checkpoint.astype(jnp.float32)
     gain_own = norm_gain.astype(jnp.float32)
-    input_full = lax.psum(partial_input.astype(jnp.bfloat16), "tensor").astype(jnp.float32)
+
+    def assign_windows(z, mesh_name):
+        spare = jax.lax.all_gather(z, mesh_name)
+        return jnp.sum(spare, axis=0)
+
+    input_full = assign_windows(partial_input.astype(jnp.bfloat16), "tensor").astype(jnp.float32)
     row_sum = jnp.sum(gain_wide * input_full * x_wide, -1, keepdims=True)
     input_own = lax.dynamic_slice_in_dim(
         input_full, lax.axis_index("tensor") * slice_width, slice_width, 1

time: 711 us -> 738 us (1.038)
  waiting for transfers between devices: 478 us -> 503 us
    psum x1 -> x0, waiting for transfers between devices: 42.7 us -> none  [on_device(): lax.psum(partial_input.astype(jnp.bfloat16), 'tensor').astype(jnp.float32)]
    all_gather x1, waiting for transfers between devices: 31.3 us -> 62.2 us  [on_device(): piece = lax.all_gather(token_grads, 'dp', axis=0, tiled=True)]
    all_gather x0 -> x1, waiting for transfers between devices: none -> 23.2 us  [assign_windows(): spare = jax.lax.all_gather(z, mesh_name)]
  transfers between devices with their start and end apart: 11 -> 11, of which waited for: 10 -> 11; matrix products, arithmetic and copies ran while one was open for 7% -> 11% of each run, Pallas kernels for 0% -> 0%
where the time goes in v1:
time: 738 us; the launch traced here: 737 us
  waiting for transfers between devices  503 us (68%)
  blocking collectives  107 us (14%)
  matrix products  55.9 us (8%)
  other arithmetic  29.5 us (4%)
  local copies, waits for them, and re-layouts  20.9 us (3%)
  between operations  14.7 us (2%)
    all_gather x1, waiting for transfers between devices, on_device(): lax.all_gather(w_query, 'dp', axis=0, tiled=True)  156 us
    all_gather x1, waiting for transfers between devices, on_device(): piece = lax.all_gather(token_grads, 'dp', axis=0, tiled=True)  62.2 us
    reduce_scatter x1, waiting for transfers between devices, on_device(): lax.psum_scatter(dkey_part.reshape(seq_length, own_kv * head_width).astyp...  61.8 us
    reduce_scatter x1, waiting for transfers between devices, on_device(): lax.psum_scatter(dvalue_part.reshape(seq_length, own_kv * head_width).ast...  49.6 us
    all_gather x1, waiting for transfers between devices, on_device(): lax.all_gather(w_value, 'dp', axis=0, tiled=True)  46.5 us
    all_gather x1, waiting for transfers between devices, on_device(): lax.all_gather(w_key, 'dp', axis=0, tiled=True)  41.7 us
    all_gather x1, blocking collectives, on_device(): lax.all_gather(value_half, 'dp', axis=0, tiled=True)  34.7 us
    all_gather x1, blocking collectives, on_device(): lax.all_gather(key_rot, 'dp', axis=0, tiled=True)  32.5 us
  transfers between devices with their start and end apart: 11, of which 11 were waited for; matrix products, arithmetic and copies ran while one was open for 11% of the time, Pallas kernels for 0%

profile of v1, /device:TPU:0, one launch (start us, length us, event | category | flops | bytes accessed | tf_op | source)
XLA Modules:
  0.0 737.2 jit_solution(17070906995359006764)
XLA Ops:
  7.2 0.7 all-gather.9.cloned.1.call-update
  7.9 0.7 all-gather.15.cloned.1.call-update
  8.7 0.7 all-gather.11.cloned.1.call-update
  9.4 0.5 all-gather.13.cloned.1.call-update
  10.0 6.4 all_gather.37
  16.4 1.9 copy.55
  18.4 0.9 multiply_cosine_fusion
  19.4 15.5 %all-gather.9.cloned.1.call-done = bf16[128,8192]{1,0:T(8,128)(2,1)} async-done(((bf16[128,2048]{1,0:T(8,128)(2,1)}), bf16[128,8192]{1,0:T(8,128)(2,1)}) %all-gather.9.cloned.1.call-update) | async-done | bytes 2097168 | tf_op jit(solution)/shard_map/all_gather | solution.py:58
  34.9 2.1 fusion.1
  36.9 0.5 multiply_multiply_fusion
  37.5 2.2 fusion.3
  39.6 46.5 %all-gather.15.cloned.1.call-done = bf16[8192,128]{1,0:T(8,128)(2,1)} async-done(((bf16[1024,128]{1,0:T(8,128)(2,1)}), bf16[8192,128]{1,0:T(8,128)(2,1)}) %all-gather.15.cloned.1.call-update) | async-done | bytes 2097168 | tf_op jit(solution)/shard_map/all_gather | solution.py:69
  86.1 2.3 fusion.90
  88.4 5.4 all_gather.43
  94.2 41.7 %all-gather.11.cloned.1.call-done = bf16[8192,128]{1,0:T(8,128)(2,1)} async-done(((bf16[1024,128]{1,0:T(8,128)(2,1)}), bf16[8192,128]{1,0:T(8,128)(2,1)}) %all-gather.11.cloned.1.call-update) | async-done | bytes 2097168 | tf_op jit(solution)/shard_map/all_gather | solution.py:68
  135.9 2.3 fusion.89
  138.2 5.8 all_gather.39
  144.2 0.3 fusion.81
  144.7 32.5 %all_gather.40 = bf16[1024,128]{1,0:T(8,128)(2,1)S(1)} all-gather(bf16[128,128]{1,0:T(8,128)(2,1)S(1)} %pad_maximum_fusion.6), channel_id=1, replica_groups=mesh['sweep'=1,'dp'=8,'tensor'=4] {'dp'}, dimensions={0}, use_global_device_ids=true | all-gather | bytes 294912 | tf_op jit(solution)/shard_map/all_gather | solution.py:103
  177.2 34.7 %all-gather = bf16[1024,128,1]{1,0,2:T(8,128)(2,1)} all-gather(bf16[128,128,1]{1,0,2:T(8,128)(2,1)S(1)} %copy.83), channel_id=2, replica_groups=mesh['sweep'=1,'dp'=8,'tensor'=4] {'dp'}, dimensions={0}, use_global_device_ids=true | all-gather | bytes 294912 | tf_op jit(solution)/shard_map/all_gather | solution.py:104
  211.9 156.1 %all-gather.13.cloned.1.call-done = bf16[8192,1024]{1,0:T(8,128)(2,1)} async-done(((bf16[1024,1024]{1,0:T(8,128)(2,1)}), bf16[8192,1024]{1,0:T(8,128)(2,1)}) %all-gather.13.cloned.1.call-update) | async-done | bytes 16777232 | tf_op jit(solution)/shard_map/all_gather | solution.py:67
  368.0 8.1 %convolution_bitcast_fusion = f32[16,8,8,128]{3,1,2,0:T(8,128)S(1)} fusion(bf16[128,8192]{1,0:T(8,128)(2,1)S(1)} %fusion.3, bf16[8192,1024]{1,0:T(8,128)(2,1)} %all-gather.13.cloned.1.call-done), kind=kOutput, calls=%fused_computation.37 | convolution fusion | flops 2147483648 | bytes 19398656 | tf_op jit(solution)/shard_map/dot_general | solution.py:75
  376.7 0.8 fusion.9
  377.5 0.9 fusion.8
  378.3 1.1 copy-done.1
  379.5 1.9 fusion.41
  381.4 0.2 reduce-scatter.5.cloned.1.call-start
  381.6 3.7 fusion.47
  385.3 1.5 fusion.6
  386.8 1.3 copy-done.5
  388.2 1.5 fusion.50
  389.7 2.5 fusion.32
  392.3 49.6 %reduce-scatter.9.cloned.1.call-done = bf16[128,128]{1,0:T(8,128)(2,1)} async-done(((bf16[1024,128]{1,0:T(8,128)(2,1)}), bf16[128,128]{1,0:T(8,128)(2,1)}) %reduce-scatter.9.cloned.1.call-update) | async-done | bytes 32784 | tf_op jit(solution)/shard_map/reduce_scatter | solution.py:149
  441.8 0.9 copy.67
  442.8 1.4 dynamic_update_slice.7
  444.2 0.6 copy-done.12
  444.9 61.8 %reduce-scatter.5.cloned.1.call-done = bf16[128,128]{1,0:T(8,128)(2,1)} async-done(((bf16[1024,128]{1,0:T(8,128)(2,1)}), bf16[128,128]{1,0:T(8,128)(2,1)}) %reduce-scatter.5.cloned.1.call-update) | async-done | bytes 32784 | tf_op jit(solution)/shard_map/reduce_scatter | solution.py:143
  506.7 0.8 bitcast_convert_fusion.1
  507.5 0.3 fusion.78
  508.1 1.4 dynamic_update_slice.6
  509.5 0.6 copy-done.11
  510.3 0.3 add_convert_fusion
  510.9 17.6 %reduce-scatter.11.cloned.1.call-done = bf16[128,128]{0,1:T(8,128)(2,1)} async-done(((bf16[128,512]{0,1:T(8,128)(2,1)}), bf16[128,128]{0,1:T(8,128)(2,1)}) %reduce-scatter.11.cloned.1.call-update) | async-done | bytes 32784 | tf_op jit(solution)/shard_map/reduce_scatter | solution.py:174
  528.4 22.7 %reduce-scatter.7.cloned.1.call-done = bf16[128,128]{0,1:T(8,128)(2,1)} async-done(((bf16[128,512]{0,1:T(8,128)(2,1)}), bf16[128,128]{0,1:T(8,128)(2,1)}) %reduce-scatter.7.cloned.1.call-update) | async-done | bytes 32784 | tf_op jit(solution)/shard_map/reduce_scatter | solution.py:171
  551.1 1.5 pad_maximum_fusion
  552.7 13.5 %fusion.91 = f32[128,8192]{1,0:T(8,128)} fusion(bf16[128,1024]{0,1:T(8,128)(2,1)S(1)} %bitcast.171, bf16[8192,1024]{1,0:T(8,128)(2,1)} %all-gather.13.cloned.1.call-done), kind=kOutput, calls=%fused_computation.102 | convolution fusion | flops 2147483648 | bytes 21233664 | tf_op jit(solution)/shard_map/tc,dc->td/dot_general | solution.py:50
  566.2 3.7 convolution_add_fusion.1
  570.0 2.1 fusion
  572.1 2.4 copy.68
  574.5 5.5 all-to-all-start
  580.1 62.2 %all-gather.17.cloned.1.call-done = bf16[1024,1280]{0,1:T(8,128)(2,1)} async-done(((bf16[128,1280]{0,1:T(8,128)(2,1)}), bf16[1024,1280]{0,1:T(8,128)(2,1)}) %all-gather.17.cloned.1.call-update) | async-done | bytes 2621456 | tf_op jit(solution)/shard_map/all_gather | solution.py:210
  642.3 3.0 copy.69
  645.2 3.6 all-to-all-done
  648.9 12.1 %convolution_convert_fusion = bf16[8,1024,1280]{2,1,0:T(8,128)(2,1)} fusion(bf16[8,128,1280]{2,1,0:T(8,128)(2,1)S(1)} %bitcast.166, bf16[128,8,1024]{0,2,1:T(8,128)(2,1)} %all-to-all-done), kind=kOutput, calls=%fused_computation.1 | convolution fusion | flops 2694840320 | bytes 25690112 | tf_op jit(solution)/shard_map/btd,btc->bdc/dot_general | solution.py:215
  661.0 11.4 %convert_reduce_fusion = f32[1024,1280]{1,0:T(8,128)S(1)} fusion(bf16[8,1024,1280]{2,1,0:T(8,128)(2,1)} %convolution_convert_fusion), kind=kLoop, calls=%fused_computation | loop fusion | flops 19660800 | bytes 26214400 | tf_op jit(solution)/shard_map/reduce_sum | solution.py:216
  672.4 2.7 slice.52
  675.0 1.0 fusion.87
  676.1 23.2 %all-gather.19.cloned.1.call-done = bf16[512,8192]{1,0:T(8,128)(2,1)} async-done(((bf16[128,8192]{1,0:T(8,128)(2,1)}), bf16[512,8192]{1,0:T(8,128)(2,1)}) %all-gather.19.cloned.1.call-update) | async-done | bytes 8388624 | tf_op jit(solution)/shard_map/all_gather | solution.py:195
  699.3 5.1 reduce_sum.72
  704.5 0.4 convert_element_type.144
  704.9 1.1 copy-done
  706.0 0.8 fusion.4
  706.8 1.4 fusion.58
  708.2 22.2 %psum.7 = f32[2048]{0:T(1024)} all-reduce(f32[2048]{0:T(1024)S(1)} %get-tuple-element.7), channel_id=1, replica_groups=mesh['sweep'=1,'dp'=8,'tensor'=4] {'dp'}, use_global_device_ids=true, to_apply=%region_11.12 | all-reduce | flops 2048 | bytes 16384 | tf_op jit(solution)/shard_map/psum | solution.py:206
  (80 shorter events, 2.5 us)
Async XLA Ops:
  7.2 27.7 %all-gather.9.cloned.1.call-start = ((), (), s32[]{:S(2)}) async-start(), calls=%async_computation.5 | async-start | bytes 2621440 | tf_op jit(solution)/shard_map/all_gather | solution.py:58
  7.9 78.2 %all-gather.15.cloned.1.call-start = ((), (), s32[]{:S(2)}) async-start(), calls=%async_computation.8 | async-start | bytes 2359296 | tf_op jit(solution)/shard_map/all_gather | solution.py:69
  8.6 127.2 %all-gather.11.cloned.1.call-start = ((), (), s32[]{:S(2)}) async-start(), calls=%async_computation.6 | async-start | bytes 2359296 | tf_op jit(solution)/shard_map/all_gather | solution.py:68
  9.4 358.6 %all-gather.13.cloned.1.call-start = ((), (), s32[]{:S(2)}) async-start(), calls=%async_computation.7 | async-start | bytes 18874368 | tf_op jit(solution)/shard_map/all_gather | solution.py:67
  10.0 431.9 %reduce-scatter.9.cloned.1.call-start = ((), (), s32[]{:S(2)}) async-start(), calls=%async_computation.11 | async-start | bytes 294912 | tf_op jit(solution)/shard_map/reduce_scatter | solution.py:149
  16.4 69.7 %copy-start.13 = (f32[8192]{0:T(1024)}, f32[8192]{0:T(1024)S(1)}, u32[]{:S(2)}) copy-start(f32[8192]{0:T(1024)S(1)} %convert_element_type.122) | copy-start | bytes 98308
  37.5 50.9 %copy-start.21 = (f32[128]{0:T(128)}, f32[128]{0:T(128)S(1)}, u32[]{:S(2)}) copy-start(f32[128]{0:T(128)S(1)} %get-tuple-element.22) | copy-start | bytes 1540
  368.0 8.4 %copy-start.6 = (f32[128,64]{1,0:T(8,128)S(1)}, f32[128,64]{1,0:T(8,128)}, u32[]{:S(2)}) copy-start(f32[128,64]{1,0:T(8,128)} %get-tuple-element.19) | copy-start | bytes 98308
  368.0 8.5 %copy-start.8 = (f32[128,64]{1,0:T(8,128)S(1)}, f32[128,64]{1,0:T(8,128)}, u32[]{:S(2)}) copy-start(f32[128,64]{1,0:T(8,128)} %get-tuple-element.20) | copy-start | bytes 98308
  376.6 2.8 copy-start.15
  377.5 2.0 copy-start.1
  379.5 2.1 copy-start.10
  381.4 125.4 %reduce-scatter.5.cloned.1.call-start = ((), (), s32[]{:S(2)}) async-start(), calls=%async_computation.9 | async-start | bytes 294912 | tf_op jit(solution)/shard_map/reduce_scatter | solution.py:143
  381.6 3.7 copy-start.2
  381.6 3.7 copy-start.16
  381.6 3.7 copy-start.17
  386.8 1.3 copy-start.5
  388.2 122.1 %copy-start.7 = (f32[128,64]{1,0:T(8,128)S(1)}, f32[128,64]{1,0:T(8,128)}, u32[]{:S(2)}) copy-start(f32[128,64]{1,0:T(8,128)} %get-tuple-element.19) | copy-start | bytes 98308
  388.2 122.1 %copy-start.9 = (f32[128,64]{1,0:T(8,128)S(1)}, f32[128,64]{1,0:T(8,128)}, u32[]{:S(2)}) copy-start(f32[128,64]{1,0:T(8,128)} %get-tuple-element.20) | copy-start | bytes 98308
  389.7 138.8 %reduce-scatter.11.cloned.1.call-start = ((), (), s32[]{:S(2)}) async-start(), calls=%async_computation.12 | async-start | bytes 163840 | tf_op jit(solution)/shard_map/reduce_scatter | solution.py:174
  444.2 0.7 copy-start.12
  444.9 106.2 %reduce-scatter.7.cloned.1.call-start = ((), (), s32[]{:S(2)}) async-start(), calls=%async_computation.10 | async-start | bytes 163840 | tf_op jit(solution)/shard_map/reduce_scatter | solution.py:171
  509.5 0.7 copy-start.11
  510.2 132.1 %all-gather.17.cloned.1.call-start = ((), (), s32[]{:S(2)}) async-start(), calls=%async_computation.13 | async-start | bytes 2949120 | tf_op jit(solution)/shard_map/all_gather | solution.py:210
  552.7 13.6 %copy-start.19 = (bf16[128,128]{0,1:T(8,128)(2,1)S(1)}, bf16[128,128]{0,1:T(8,128)(2,1)}, u32[]{:S(2)}) copy-start(bf16[128,128]{0,1:T(8,128)(2,1)} %reduce-scatter.7.cloned.1.call-done) | copy-start | bytes 98308
  552.7 146.6 %all-gather.19.cloned.1.call-start = ((), (), s32[]{:S(2)}) async-start(), calls=%async_computation.14 | async-start | bytes 10485760 | tf_op jit(solution)/shard_map/all_gather | solution.py:195
  566.2 3.7 copy-start.3
  566.2 3.7 copy-start.18
  572.0 8.0 %copy-start.20 = (bf16[2048]{0:T(1024)(128)(2,1)S(1)}, bf16[2048]{0:T(1024)(128)(2,1)}, u32[]{:S(2)}) copy-start(bf16[2048]{0:T(1024)(128)(2,1)} %param.7) | copy-start | bytes 12292
  574.5 74.4 %all-to-all-start = ((bf16[128,8,1024]{0,2,1:T(8,128)(2,1)}), bf16[128,8,1024]{0,2,1:T(8,128)(2,1)}, u32[]{:S(2)}, u32[]{:S(2)}) async-start(bf16[128,8,1024]{0,2,1:T(8,128)(2,1)} %bitcast.168), calls=%async_computation.4 | async-start | bytes 4194304 | tf_op jit(solution)/shard_map/all_to_all | solution.py:209
  704.4 1.6 copy-start
  704.4 1.6 copy-start.14
  704.4 2.4 copy-start.4
  704.4 2.4 copy-start.22
  704.4 2.4 copy-start.23
Sparse Core Ops, SparseCore 0:
  9.5 25.2 all-gather.8
  37.0 49.0 all-gather.14
  88.2 47.6 all-gather.10
  137.9 230.0 all-gather.12
  381.5 60.3 reduce-scatter.8
  445.6 61.0 reduce-scatter.4
  509.7 18.6 reduce-scatter.10
  531.4 19.6 reduce-scatter.6
  553.7 88.4 all-gather.16
  643.7 55.5 all-gather.18
